TPU v7x, 32 devices: a whole 2x2x4 slice. The times are simulated.
32 devices in a mesh: ep: 8 (over z, x), dp: 4 (over y, core).
Axes of the slice: x: 2, y: 2, z: 4, core: 2. Of those that a mesh axis runs over, the one named last changes fastest.
Arguments:
- residual: bfloat16 [4096, 2880], P(('ep', 'dp')), may hold values from -400 to 400, as said below
- norm_gain: float32 [2880], replicated, may hold values from 0.25 to 1.75
- router_weight: bfloat16 [2880, 32], replicated, may hold values from -0.109375 to 0.109375
- out_grad: bfloat16 [4096, 2880], P(('ep', 'dp')), may hold values from -6 to 6
- expert_ids: int32 [4096, 4], P(('ep', 'dp')), may hold values from 0 to 31, all different within a row; in each aligned block of 128 rows (0 to 127, 128 to 255, ...) at most 24 rows name the same one
- hidden: bfloat16 [32, 768, 1440], P(('ep', 'dp')), may hold values from -0.3125 to 0.3125
- down_weight: bfloat16 [32, 1440, 2880], P(('ep', 'dp')), may hold values from -0.15625 to 0.15625
Outputs:
- hidden_grad: bfloat16 [32, 768, 1440], P(('ep', 'dp'))
- down_weight_grad: bfloat16 [32, 1440, 2880], P(('ep', 'dp'))
- residual_grad: bfloat16 [4096, 2880], P(('ep', 'dp'))
- router_grad: float32 [2880, 32], replicated
- gain_grad: float32 [2880], replicated
Inputs may be any that keep to these rules, and one draw needn't show every extreme that they name: `expert_ids`: in the tokens of one device no expert is named more than 24 times, a bound that some block reaches. `residual`: Real-valued entries.
All inputs are finite; a program needn't handle non-finite values.
Results may differ from a plain program's by a relative error of at most 0.0085.
Values may be sent and summed in bfloat16 or wider, within the bound.
A program may use at most 128 MiB of HBM per device.

v0:
```python
import jax
import jax.numpy as jnp
from jax import lax
from jax.sharding import PartitionSpec as P


def on_device(residual, norm_gain, router_weight, out_grad, expert_ids, hidden, down_weight):
    tokens_here, width = residual.shape
    top_count = expert_ids.shape[1]
    experts = router_weight.shape[1]
    slots = hidden.shape[1]
    capacity = slots // experts
    floated = residual.astype(jnp.float32)
    inverse = lax.rsqrt(jnp.mean(floated * floated, -1, keepdims=True) + 1e-05)
    unit = floated * inverse
    normed = (unit * norm_gain).astype(jnp.bfloat16)
    logits = jnp.dot(normed, router_weight, preferred_element_type=jnp.float32)
    match = expert_ids[:, :, None] == jnp.arange(experts, dtype=jnp.int32)[None, None, :]
    picked = jnp.sum(jnp.where(match, logits[:, None, :], jnp.float32(0.0)), -1)
    expo = jnp.exp(picked)
    prob = expo / jnp.sum(expo, -1, keepdims=True)
    flat_ids = expert_ids.reshape(-1)
    onehot = (flat_ids[:, None] == jnp.arange(experts, dtype=jnp.int32)[None, :]).astype(jnp.int32)
    slot_rank = jnp.sum((jnp.cumsum(onehot, 0) - onehot) * onehot, -1)
    place = flat_ids * capacity + slot_rank
    repeated = jnp.repeat(out_grad, top_count, axis=0)
    send_rows = jnp.zeros((experts * capacity, width), jnp.bfloat16).at[place].set(repeated)
    send_prob = (
        jnp.zeros((experts * capacity,), jnp.bfloat16)
        .at[place]
        .set(prob.astype(jnp.bfloat16).reshape(-1))
    )
    got_rows, got_prob = (
        lax.all_to_all(send_rows, ("ep", "dp"), split_axis=0, concat_axis=0, tiled=True),
        lax.all_to_all(send_prob, ("ep", "dp"), split_axis=0, concat_axis=0, tiled=True),
    )
    hidden_rows = hidden[0]
    weight = down_weight[0]
    inner = lax.dot_general(
        got_rows, weight, (((1,), (1,)), ((), ())), preferred_element_type=jnp.float32
    )
    slot_score = jnp.sum(inner * hidden_rows.astype(jnp.float32), -1)
    weight_col = got_prob.astype(jnp.float32)[:, None]
    hidden_grad = (weight_col * inner).astype(jnp.bfloat16)
    scaled = (weight_col * got_rows.astype(jnp.float32)).astype(jnp.bfloat16)
    weight_grad = lax.dot_general(
        hidden_rows, scaled, (((0,), (0,)), ((), ())), preferred_element_type=jnp.float32
    )
    came_back = lax.all_to_all(slot_score, ("ep", "dp"), split_axis=0, concat_axis=0, tiled=True)
    score = came_back[place].reshape(tokens_here, top_count)
    pick_grad = prob * (score - jnp.sum(prob * score, -1, keepdims=True))
    logit_grad = jnp.sum(jnp.where(match, pick_grad[:, :, None], jnp.float32(0.0)), 1)
    local_router = jnp.dot(
        normed.astype(jnp.float32).T, logit_grad, precision=lax.Precision.HIGHEST
    )
    normed_grad = jnp.dot(
        logit_grad, router_weight.astype(jnp.float32).T, precision=lax.Precision.HIGHEST
    )
    local_gain = jnp.sum(normed_grad * unit, 0)
    router_grad, gain_grad = lax.psum((local_router, local_gain), ("ep", "dp"))
    upper = normed_grad * norm_gain
    residual_grad = (inverse * (upper - unit * jnp.mean(upper * unit, -1, keepdims=True))).astype(
        jnp.bfloat16
    )
    return (
        hidden_grad[None],
        weight_grad.astype(jnp.bfloat16)[None],
        residual_grad,
        router_grad,
        gain_grad,
    )


def solution(mesh):
    return jax.shard_map(
        on_device,
        mesh=mesh,
        in_specs=(
            P(("ep", "dp"), None),
            P(),
            P(),
            P(("ep", "dp"), None),
            P(("ep", "dp"), None),
            P(("ep", "dp"), None, None),
            P(("ep", "dp"), None, None),
        ),
        out_specs=(
            P(("ep", "dp"), None, None),
            P(("ep", "dp"), None, None),
            P(("ep", "dp"), None),
            P(),
            P(),
        ),
        check_vma=False,
    )
```

profile of v0, /device:TPU:0, one launch (start us, length us, event | category | flops | bytes accessed | tf_op | source)
XLA Modules:
  0.0 325.0 jit_solution(3421626252912884726)
XLA Ops:
  7.2 0.8 broadcast_multiply_fusion
  8.0 0.8 copy.37
  9.0 0.1 copy.36
  9.2 1.2 reduce-window.6
  10.4 0.2 slice_reduce_fusion
  10.6 1.5 fusion.17
  12.2 1.7 fusion.20
  13.9 0.1 copy.40
  14.1 0.1 reshape.161
  14.3 3.8 %scatter_custom_fusion = bf16[768]{0:T(1024)(128)(2,1)S(1)} fusion(s32[512]{0:T(512)S(1)} %bitcast.53, bf16[512]{0:T(512)(128)(2,1)S(1)} %reshape.161, bf16[]{:T(256)} %constant.7.clone.1), kind=kCustom, calls=%fused_computation.49 | custom fusion | bytes 1538 | tf_op jit(solution)/shard_map/scatter | solution.py:31
  18.1 0.7 all_to_all.30
  18.8 7.3 %all-to-all-start = ((bf16[32,24,1]{1,2,0:T(2,128)(2,1)}), bf16[32,24,1]{1,2,0:T(2,128)(2,1)S(1)}, u32[]{:S(2)}, u32[]{:S(2)}) async-start(bf16[32,24,1]{1,2,0:T(2,128)(2,1)} %all_to_all.30), calls=%async_computation | async-start | bytes 32768 | tf_op jit(solution)/shard_map/all_to_all | solution.py:35
  26.1 1.2 copy.44
  27.3 1.9 broadcast_in_dim.56
  29.2 2.9 reshape.169
  32.1 8.8 %scatter_custom_fusion.1 = bf16[768,2880]{1,0:T(8,128)(2,1)} fusion(s32[512]{0:T(512)S(1)} %bitcast.54, bf16[512,2880]{1,0:T(8,128)(2,1)} %reshape.169, bf16[]{:T(256)} %constant.7.clone.1), kind=kCustom, calls=%fused_computation.10 | custom fusion | bytes 4424192 | tf_op jit(solution)/shard_map/scatter | solution.py:27
  40.9 5.9 %all-to-all-start.1 = ((bf16[32,24,2880]{2,1,0:T(8,128)(2,1)}), bf16[32,24,2880]{2,1,0:T(8,128)(2,1)}, u32[]{:S(2)}, u32[]{:S(2)}) async-start(bf16[32,24,2880]{2,1,0:T(8,128)(2,1)} %bitcast.51), calls=%async_computation.1 | async-start | bytes 9043968 | tf_op jit(solution)/shard_map/all_to_all | solution.py:34
  47.2 100.9 %all-to-all-done.1 = bf16[32,24,2880]{2,1,0:T(8,128)(2,1)} async-done(((bf16[32,24,2880]{2,1,0:T(8,128)(2,1)}), bf16[32,24,2880]{2,1,0:T(8,128)(2,1)}, u32[]{:S(2)}, u32[]{:S(2)}) %all-to-all-start.1) | async-done | bytes 4423712 | tf_op jit(solution)/shard_map/all_to_all | solution.py:34
  148.1 12.2 %multiply_reduce_fusion = (f32[768]{0:T(1024)S(1)}, bf16[1,768,1440]{1,2,0:T(8,128)(2,1)}) fusion(bf16[1,768,1440]{1,2,0:T(8,128)(2,1)} %param.12, f32[768]{0:T(1024)S(1)} %reshape.147, bf16[768,2880]{1,0:T(8,128)(2,1)} %bitcast.4, bf16[1,1440,2880]{2,1,0:T(8,128)(2,1)} %param.13), kind=kOutput, calls=%fused_computation.8 | convolution fusion | flops 6375627776 | bytes 17147904 | tf_op jit(solution)/shard_map/dot_general | solution.py:39
  160.3 0.7 all_to_all.27
  161.0 5.2 %all-to-all-start.2 = ((f32[32,24,1]{1,2,0:T(1,128)}), f32[32,24,1]{1,2,0:T(1,128)S(1)}, u32[]{:S(2)}, u32[]{:S(2)}) async-start(f32[32,24,1]{1,2,0:T(1,128)} %bitcast.12), calls=%async_computation.2 | async-start | bytes 32768 | tf_op jit(solution)/shard_map/all_to_all | solution.py:49
  166.3 3.8 %multiply_convert_fusion = bf16[32,24,2880]{2,1,0:T(8,128)(2,1)S(1)} fusion(bf16[32,24,2880]{2,1,0:T(8,128)(2,1)} %all-to-all-done.1, f32[32,24]{1,0:T(8,128)S(1)} %copy.45), kind=kLoop, calls=%fused_computation.5 | loop fusion | flops 6635520 | bytes 8850432 | tf_op jit(solution)/shard_map/convert_element_type | solution.py:45
  170.1 9.3 %fusion = bf16[1,1440,2880]{2,1,0:T(8,128)(2,1)} fusion(bf16[768,2880]{1,0:T(8,128)(2,1)S(1)} %bitcast.52, bf16[1,768,1440]{1,2,0:T(8,128)(2,1)S(1)} %copy-done.5), kind=kOutput, calls=%fused_computation.4 | convolution fusion | flops 6374246400 | bytes 14929920 | tf_op jit(solution)/shard_map/dot_general | solution.py:46
  179.4 0.5 broadcast.113
  179.9 0.7 reduce.5
  180.7 2.3 gather_fusion
  183.3 1.7 fusion.16
  184.9 1.8 fusion.18
  186.8 1.3 fusion.15
  188.1 40.6 %psum.15 = f32[2880]{0:T(1024)} all-reduce(f32[2880]{0:T(1024)S(1)} %get-tuple-element.5), channel_id=1, replica_groups=mesh['ep'=8,'dp'=4] {'ep','dp'}, use_global_device_ids=true, to_apply=%region_14.15 | all-reduce | flops 2880 | bytes 23040 | tf_op jit(solution)/shard_map/psum | solution.py:60
  228.7 87.7 %all-reduce.2.cloned.1.call-done = f32[2880,32]{0,1:T(8,128)} async-done(((f32[2880,32]{0,1:T(8,128)}), f32[2880,32]{0,1:T(8,128)}) %all-reduce.2.cloned.1.call-update) | async-done | bytes 368656 | tf_op jit(solution)/shard_map/psum | solution.py:60
  316.4 1.8 copy.52
  (41 shorter events, 1.3 us)
Async XLA Ops:
  7.2 5.0 %copy-start = (bf16[2880,32]{0,1:T(8,128)(2,1)S(1)}, bf16[2880,32]{0,1:T(8,128)(2,1)}, u32[]{:S(2)}) copy-start(bf16[2880,32]{0,1:T(8,128)(2,1)} %param.9) | copy-start | bytes 552964
  7.2 6.7 %copy-start.3 = (s32[128,4]{0,1:T(4,128)S(1)}, s32[128,4]{0,1:T(4,128)}, u32[]{:S(2)}) copy-start(s32[128,4]{0,1:T(4,128)} %param.11) | copy-start | bytes 6148
  7.2 18.9 %copy-start.2 = (bf16[128,2880]{0,1:T(8,128)(2,1)S(1)}, bf16[128,2880]{0,1:T(8,128)(2,1)}, u32[]{:S(2)}) copy-start(bf16[128,2880]{0,1:T(8,128)(2,1)} %param.10) | copy-start | bytes 2211844
  18.8 22.1 %all-to-all-start = ((bf16[32,24,1]{1,2,0:T(2,128)(2,1)}), bf16[32,24,1]{1,2,0:T(2,128)(2,1)S(1)}, u32[]{:S(2)}, u32[]{:S(2)}) async-start(bf16[32,24,1]{1,2,0:T(2,128)(2,1)} %all_to_all.30), calls=%async_computation | async-start | bytes 32768 | tf_op jit(solution)/shard_map/all_to_all | solution.py:35
  40.9 107.3 %all-to-all-start.1 = ((bf16[32,24,2880]{2,1,0:T(8,128)(2,1)}), bf16[32,24,2880]{2,1,0:T(8,128)(2,1)}, u32[]{:S(2)}, u32[]{:S(2)}) async-start(bf16[32,24,2880]{2,1,0:T(8,128)(2,1)} %bitcast.51), calls=%async_computation.1 | async-start | bytes 9043968 | tf_op jit(solution)/shard_map/all_to_all | solution.py:34
  161.0 18.4 %all-to-all-start.2 = ((f32[32,24,1]{1,2,0:T(1,128)}), f32[32,24,1]{1,2,0:T(1,128)S(1)}, u32[]{:S(2)}, u32[]{:S(2)}) async-start(f32[32,24,1]{1,2,0:T(1,128)} %bitcast.12), calls=%async_computation.2 | async-start | bytes 32768 | tf_op jit(solution)/shard_map/all_to_all | solution.py:49
  166.2 150.2 %all-reduce.2.cloned.1.call-start = ((), (), s32[]{:S(2)}) async-start(), calls=%async_computation.3 | async-start | bytes 753664 | tf_op jit(solution)/shard_map/psum | solution.py:60
  166.3 3.9 %copy-start.5 = (bf16[1,768,1440]{1,2,0:T(8,128)(2,1)S(1)}, bf16[1,768,1440]{1,2,0:T(8,128)(2,1)}, u32[]{:S(2)}) copy-start(bf16[1,768,1440]{1,2,0:T(8,128)(2,1)} %param.12) | copy-start | bytes 6635524
  179.4 3.8 %copy-start.1 = (bf16[128,2880]{0,1:T(8,128)(2,1)S(1)}, bf16[128,2880]{0,1:T(8,128)(2,1)}, u32[]{:S(2)}) copy-start(bf16[128,2880]{0,1:T(8,128)(2,1)} %param.7) | copy-start | bytes 2211844
  179.4 3.9 %copy-start.4 = (f32[2880]{0:T(1024)S(1)}, f32[2880]{0:T(1024)}, u32[]{:S(2)}) copy-start(f32[2880]{0:T(1024)} %param.8) | copy-start | bytes 34564
Sparse Core Ops, SparseCore 0:
  186.9 129.4 all-reduce.1
where the time goes:
time: 326 us; the launch traced here: 325 us
  waiting for transfers between devices  189 us (58%)
  blocking collectives  40.6 us (12%)
  local copies, waits for them, and re-layouts  26.7 us (8%)
  matrix products  26.6 us (8%)
  starting transfers between devices  18.5 us (6%)
  between operations  14.3 us (4%)
  other arithmetic  9.59 us (3%)
    all_to_all x1, waiting for transfers between devices, on_device(): lax.all_to_all(send_rows, ('ep', 'dp'), split_axis=0, concat_axis=0, tile...  101 us
    psum x1, waiting for transfers between devices, on_device(): router_grad, gain_grad = lax.psum((local_router, local_gain), ('ep', 'dp'))  87.7 us
    psum x1, blocking collectives, on_device(): router_grad, gain_grad = lax.psum((local_router, local_gain), ('ep', 'dp'))  40.6 us
    dot_general x1, matrix products, on_device(): lax.dot_general(got_rows, weight, (((1,), (1,)), ((), ())), preferred_ele...  12.2 us
    dot_general x1, matrix products, on_device(): lax.dot_general(hidden_rows, scaled, (((0,), (0,)), ((), ())), preferred_...  9.29 us
    scatter x1, local copies, waits for them, and re-layouts, on_device(): jnp.zeros((experts * capacity, width), jnp.bfloat16).at[place].set(repeated)  8.78 us
    all_to_all x1, starting transfers between devices, on_device(): lax.all_to_all(send_prob, ('ep', 'dp'), split_axis=0, concat_axis=0, tile...  7.33 us
  transfers between devices with their start and end apart: 4, of which 2 were waited for; matrix products, arithmetic and copies ran while one was open for 9% of the time, Pallas kernels for 0%

commit v1 on v0

v1 whole, which is shorter than its diff:
```python
import functools

import jax
import jax.numpy as jnp
from jax import lax
from jax.experimental import pallas as pl
from jax.experimental.pallas import tpu as pltpu
from jax.sharding import PartitionSpec as P

F32 = jnp.float32
BF16 = jnp.bfloat16


def kernel(
    n_ep, n_dp, cap,
    res_ref, gain_ref, rwt_ref, og_ref, ids_ref, hid_any, w_any,
    hg_any, wg_any, rg_ref, rgt_ref, gg_ref,
    send, recv, w, hid, hidt, scaled, hg, wg, normed_s, unit_s, inv_s, prob_s, rank_s, rankt_s, probt_s,
    ssend, srecv, part, rsbuf, agbuf,
    in_sem, row_send, row_recv, sc_send, sc_recv, rs_send, rs_recv, ag_send, ag_recv, hg_sem, wg_sem,
):
    n = n_ep * n_dp
    tokens, width = res_ref.shape
    experts = rwt_ref.shape[0]
    ff = w.shape[0]
    pad_width = send.shape[2]
    group = n_dp * cap
    ep = lax.axis_index("ep")
    dp = lax.axis_index("dp")
    me = ep * n_dp + dp

    def remote(src, dst, s_sem, r_sem, dev_ep, dev_dp):
        return pltpu.make_async_remote_copy(
            src_ref=src, dst_ref=dst, send_sem=s_sem, recv_sem=r_sem,
            device_id=(dev_ep, dev_dp), device_id_type=pl.DeviceIdType.MESH,
        )

    barrier = pltpu.get_barrier_semaphore()

    def greet(i, _):
        @pl.when(i != me)
        def _():
            pl.semaphore_signal(
                barrier, inc=1, device_id=(i // n_dp, i % n_dp), device_id_type=pl.DeviceIdType.MESH
            )
        return 0

    lax.fori_loop(0, n, greet, 0)
    load_h = pltpu.make_async_copy(hid_any, hid, in_sem.at[0])
    load_w = pltpu.make_async_copy(w_any, w, in_sem.at[1])
    load_h.start()
    load_w.start()

    floated = res_ref[...].astype(F32)
    inverse = lax.rsqrt(jnp.mean(floated * floated, -1, keepdims=True) + 1e-05)
    unit = floated * inverse
    normed = (unit * gain_ref[...]).astype(BF16)
    unit_s[...] = unit
    inv_s[...] = inverse
    normed_s[...] = normed
    logits = lax.dot_general(
        normed, rwt_ref[...], (((1,), (1,)), ((), ())), preferred_element_type=F32
    )
    lane_e = lax.broadcasted_iota(jnp.int32, (tokens, experts), 1)
    match = jnp.zeros((tokens, experts), F32)
    ids = ids_ref[...]
    for k in range(ids.shape[1]):
        match = match + jnp.where(ids[:, k : k + 1] == lane_e, F32(1.0), F32(0.0))
    expo = jnp.where(match > 0, jnp.exp(logits), F32(0.0))
    prob = expo / jnp.sum(expo, -1, keepdims=True)
    row_t = lax.broadcasted_iota(jnp.int32, (tokens, tokens), 0)
    col_t = lax.broadcasted_iota(jnp.int32, (tokens, tokens), 1)
    lower = jnp.where(col_t < row_t, F32(1.0), F32(0.0)).astype(BF16)
    rank = jnp.dot(lower, match.astype(BF16), preferred_element_type=F32)
    rank = jnp.where(match > 0, rank, F32(-1.0))
    prob_s[...] = prob
    rank_s[...] = rank
    rankt_s[...] = rank.T.reshape(experts, 1, tokens)
    probt_s[...] = prob.T.reshape(experts, 1, tokens)

    pl.semaphore_wait(barrier, n - 1)

    def pack(g, _):
        to = lax.rem(ep + n_ep - 1 - g, n_ep)
        first = to * n_dp
        rt = rankt_s[pl.ds(first, n_dp)]
        pt = probt_s[pl.ds(first, n_dp)]
        slot = lax.broadcasted_iota(jnp.int32, (n_dp, cap, tokens), 1).astype(F32)
        hit = slot == rt
        hot = jnp.where(hit, F32(1.0), F32(0.0)).reshape(group, tokens).astype(BF16)
        weight = jnp.sum(jnp.where(hit, pt, F32(0.0)), -1, keepdims=True)
        rows = jnp.dot(hot, og_ref[...], preferred_element_type=F32)
        send[pl.ds(first, n_dp), :, pl.ds(0, width)] = rows.reshape(n_dp, cap, width).astype(BF16)
        send[pl.ds(first, n_dp), :, pl.ds(width, pad_width - width)] = jnp.broadcast_to(
            weight, (n_dp, cap, pad_width - width)
        ).astype(BF16)
        for k in range(n_dp):
            j = lax.rem(dp + k, n_dp)
            e = first + j

            @pl.when(e != me)
            def _():
                remote(
                    send.at[e], recv.at[me], row_send.at[e], row_recv.at[me], to, j
                ).start()

            @pl.when(e == me)
            def _():
                recv[me] = send[me]
        return 0

    lax.fori_loop(0, n_ep, pack, 0)

    load_h.wait()
    hidt[...] = hid[...].T
    load_w.wait()

    def wait_rows(src_ep):
        for k in range(n_dp):
            s = src_ep * n_dp + k

            @pl.when(s != me)
            def _():
                remote(send.at[s], recv.at[s], row_send.at[s], row_recv.at[s], src_ep, k).wait_recv()

    def take(src_ep):
        got = recv[pl.ds(src_ep * n_dp, n_dp)].astype(F32)
        return got.reshape(group, pad_width)

    def chunk(c, _):
        sources = (
            lax.rem(ep + 1 + 2 * c, n_ep),
            lax.rem(ep + 2 + 2 * c, n_ep),
        )
        for s in sources:
            wait_rows(s)
        rows = jnp.concatenate([take(s) for s in sources], 0)
        starts = [pl.multiple_of(s * group, group) for s in sources]
        h = jnp.concatenate([hid[pl.ds(b, group)] for b in starts], 0).astype(F32)
        grad = rows[:, :width]
        weight = rows[:, width : width + 1]
        inner = lax.dot_general(
            grad.astype(BF16), w[...], (((1,), (1,)), ((), ())), preferred_element_type=F32
        )
        score = jnp.sum(inner * h, -1, keepdims=True).reshape(2 * n_dp, cap, 1)
        at_row = lax.broadcasted_iota(jnp.int32, (2 * n_dp, cap, 128), 1)
        at_lane = lax.broadcasted_iota(jnp.int32, (2 * n_dp, cap, 128), 2)
        score = jnp.sum(jnp.where(at_row == at_lane, score, F32(0.0)), 1, keepdims=True)
        for i, s in enumerate(sources):
            ssend[pl.ds(s * n_dp, n_dp)] = score[i * n_dp : (i + 1) * n_dp]
            for k in range(n_dp):
                d = s * n_dp + k

                @pl.when(d != me)
                def _():
                    remote(ssend.at[d], srecv.at[me], sc_send.at[d], sc_recv.at[me], s, k).start()

                @pl.when(d == me)
                def _():
                    srecv[me] = ssend[me]

        hgrad = (weight * inner).astype(BF16)
        scale = (weight * grad).astype(BF16)
        for i, s in enumerate(sources):
            hg[pl.ds(starts[i], group)] = hgrad[i * group : (i + 1) * group]
            scaled[pl.ds(starts[i], group)] = scale[i * group : (i + 1) * group]
            pltpu.make_async_copy(
                hg.at[pl.ds(starts[i], group)], hg_any.at[pl.ds(starts[i], group)], hg_sem.at[s]
            ).start()
        return 0

    lax.fori_loop(0, n_ep // 2, chunk, 0)

    blocks = wg_sem.shape[0]
    rows_of = ff // blocks

    def wg_block(b, _):
        at = pl.ds(pl.multiple_of(b * rows_of, rows_of), rows_of)
        wg[at] = jnp.dot(hidt[at], scaled[...], preferred_element_type=F32).astype(BF16)
        pltpu.make_async_copy(wg.at[at], wg_any.at[at], wg_sem.at[b]).start()
        return 0

    def others(fn):
        def step(i, _):
            @pl.when(i != me)
            def _():
                fn(i)
            return 0
        lax.fori_loop(0, n, step, 0)

    cut1, cut2 = blocks // 5, (3 * blocks) // 5
    lax.fori_loop(0, cut1, wg_block, 0)

    others(lambda i: remote(ssend.at[i], srecv.at[i], sc_send.at[i], sc_recv.at[i], i // n_dp, i % n_dp).wait_recv())
    back = srecv[...].reshape(n, 128).T
    rank = rank_s[...]
    prob = prob_s[...]
    score = jnp.zeros((tokens, experts), F32)
    for r in range(cap):
        score = score + jnp.where(rank == F32(r), back[r : r + 1, :], F32(0.0))
    lg = prob * (score - jnp.sum(prob * score, -1, keepdims=True))
    lgt = lg.T
    hit = lgt.astype(BF16)
    lot = (lgt - hit.astype(F32)).astype(BF16)
    both = jnp.dot(jnp.concatenate([hit, lot], 0), normed_s[...], preferred_element_type=F32)
    router = both[:experts] + both[experts:]
    for e in range(experts):
        part[e] = router[e : e + 1, :]
    rsbuf[me] = part[me]
    others(lambda i: remote(part.at[i], rsbuf.at[me], rs_send.at[i], rs_recv.at[me], i // n_dp, i % n_dp).start())

    lax.fori_loop(cut1, cut2, wg_block, 0)

    others(lambda i: remote(part.at[i], rsbuf.at[i], rs_send.at[i], rs_recv.at[i], i // n_dp, i % n_dp).wait_recv())
    agbuf[me] = jnp.sum(rsbuf[...], 0)
    others(lambda i: remote(agbuf.at[me], agbuf.at[me], ag_send.at[i], ag_recv.at[me], i // n_dp, i % n_dp).start())

    hi = lg.astype(BF16)
    lo = (lg - hi.astype(F32)).astype(BF16)
    rwt = rwt_ref[...]
    ngrad = jnp.dot(hi, rwt, preferred_element_type=F32) + jnp.dot(lo, rwt, preferred_element_type=F32)
    upper = ngrad * gain_ref[...]
    unit = unit_s[...]
    mean = jnp.mean(upper * unit, -1, keepdims=True)
    rg_ref[...] = (inv_s[...] * (upper - unit * mean)).astype(BF16)

    lax.fori_loop(cut2, blocks, wg_block, 0)

    others(lambda i: remote(agbuf.at[me], agbuf.at[i], ag_send.at[i], ag_recv.at[i], i // n_dp, i % n_dp).wait_recv())
    total = agbuf[...].reshape(experts, width)
    rgt_ref[...] = total
    gg_ref[...] = jnp.sum(total * rwt.astype(F32), 0, keepdims=True) / gain_ref[...]

    def finish(i):
        remote(send.at[i], recv.at[me], row_send.at[i], row_recv.at[me], i // n_dp, i % n_dp).wait_send()
        remote(ssend.at[i], srecv.at[me], sc_send.at[i], sc_recv.at[me], i // n_dp, i % n_dp).wait_send()
        remote(part.at[i], rsbuf.at[me], rs_send.at[i], rs_recv.at[me], i // n_dp, i % n_dp).wait_send()
        remote(agbuf.at[me], agbuf.at[me], ag_send.at[i], ag_recv.at[me], i // n_dp, i % n_dp).wait_send()

    others(finish)

    def drain_h(g, _):
        at = pl.ds(pl.multiple_of(g * group, group), group)
        pltpu.make_async_copy(hg.at[at], hg_any.at[at], hg_sem.at[g]).wait()
        return 0

    lax.fori_loop(0, n_ep, drain_h, 0)

    def drain_w(b, _):
        at = pl.ds(pl.multiple_of(b * rows_of, rows_of), rows_of)
        pltpu.make_async_copy(wg.at[at], wg_any.at[at], wg_sem.at[b]).wait()
        return 0

    lax.fori_loop(0, blocks, drain_w, 0)


def on_device(n_ep, n_dp, residual, norm_gain, router_weight, out_grad, expert_ids, hidden, down_weight):
    n = n_ep * n_dp
    tokens, width = residual.shape
    experts = router_weight.shape[1]
    slots, ff = hidden.shape[1:]
    real_cap = slots // experts
    cap = -(-real_cap // 8) * 8
    pad_width = -(-(width + 1) // 128) * 128
    hid = hidden[0]
    if cap != real_cap:
        hid = jnp.pad(
            hid.reshape(experts, real_cap, ff), ((0, 0), (0, cap - real_cap), (0, 0))
        ).reshape(experts * cap, ff)
    rows = experts * cap
    blocks = max(b for b in range(1, 6) if ff % (b * 16) == 0)
    vmem = pl.BlockSpec(memory_space=pltpu.VMEM)
    anyspace = pl.BlockSpec(memory_space=pl.ANY)
    dma = pltpu.SemaphoreType.DMA
    hg, wg, rg, rgt, gg = pl.pallas_call(
        functools.partial(kernel, n_ep, n_dp, cap),
        out_shape=(
            jax.ShapeDtypeStruct((rows, ff), BF16),
            jax.ShapeDtypeStruct((ff, width), BF16),
            jax.ShapeDtypeStruct((tokens, width), BF16),
            jax.ShapeDtypeStruct((experts, width), F32),
            jax.ShapeDtypeStruct((1, width), F32),
        ),
        in_specs=[vmem] * 5 + [anyspace] * 2,
        out_specs=(anyspace, anyspace, vmem, vmem, vmem),
        scratch_shapes=[
            pltpu.VMEM((n, cap, pad_width), BF16),
            pltpu.VMEM((n, cap, pad_width), BF16),
            pltpu.VMEM((ff, width), BF16),
            pltpu.VMEM((rows, ff), BF16),
            pltpu.VMEM((ff, rows), BF16),
            pltpu.VMEM((rows, width), BF16),
            pltpu.VMEM((rows, ff), BF16),
            pltpu.VMEM((ff, width), BF16),
            pltpu.VMEM((tokens, width), BF16),
            pltpu.VMEM((tokens, width), F32),
            pltpu.VMEM((tokens, 1), F32),
            pltpu.VMEM((tokens, experts), F32),
            pltpu.VMEM((tokens, experts), F32),
            pltpu.VMEM((experts, 1, tokens), F32),
            pltpu.VMEM((experts, 1, tokens), F32),
            pltpu.VMEM((n, 1, 128), F32),
            pltpu.VMEM((n, 1, 128), F32),
            pltpu.VMEM((n, 1, width), F32),
            pltpu.VMEM((n, 1, width), F32),
            pltpu.VMEM((n, 1, width), F32),
            dma((2,)),
            dma((n,)), dma((n,)), dma((n,)), dma((n,)),
            dma((n,)), dma((n,)), dma((n,)), dma((n,)),
            dma((n_ep,)),
            dma((blocks,)),
        ],
        compiler_params=pltpu.CompilerParams(
            collective_id=0, has_side_effects=True, vmem_limit_bytes=60 * 1024 * 1024
        ),
        name="expert_backward",
    )(residual, norm_gain[None], router_weight.T, out_grad, expert_ids, hid, down_weight[0])
    if cap != real_cap:
        hg = hg.reshape(experts, cap, ff)[:, :real_cap].reshape(slots, ff)
    return hg[None], wg[None], rg, rgt.T, gg[0]


def solution(mesh):
    both = ("ep", "dp")
    return jax.shard_map(
        functools.partial(on_device, mesh.shape["ep"], mesh.shape["dp"]),
        mesh=mesh,
        in_specs=(P(both, None), P(), P(), P(both, None), P(both, None), P(both, None, None), P(both, None, None)),
        out_specs=(P(both, None, None), P(both, None, None), P(both, None), P(), P()),
        check_vma=False,
    )
```

time: 326 us -> 175 us (0.54)
  waiting for transfers between devices: 189 us -> 0 us
  Pallas kernels: 0 us -> 150 us
  blocking collectives: 40.6 us -> 0 us
  matrix products: 26.6 us -> 0 us
  starting transfers between devices: 18.5 us -> 0 us
  between operations: 14.3 us -> 0.67 us
  other arithmetic: 9.59 us -> 0.63 us
    pallas_call x0 -> x1, Pallas kernels: none -> 150 us  [on_device(): pl.pallas_call(functools.partial(kernel, n_ep, n_dp, cap), out_shape=(jax...]
    all_to_all x3 -> x0, waiting for transfers between devices: 101 us -> none  [the longest x1 101 us: on_device(): lax.all_to_all(send_rows, ('ep', 'dp'), split_axis=0, concat_axis=0, tile...]
    psum x1 -> x0, waiting for transfers between devices: 87.7 us -> none  [on_device(): router_grad, gain_grad = lax.psum((local_router, local_gain), ('ep', 'dp'))]
    psum x1 -> x0, blocking collectives: 40.6 us -> none  [on_device(): router_grad, gain_grad = lax.psum((local_router, local_gain), ('ep', 'dp'))]
    dot_general x5 -> x0, matrix products: 26.6 us -> none  [the longest x1 12.2 us: on_device(): lax.dot_general(got_rows, weight, (((1,), (1,)), ((), ())), preferred_ele...]
    all_to_all x3 -> x0, starting transfers between devices: 18.4 us -> none  [the longest x1 7.33 us: on_device(): lax.all_to_all(send_prob, ('ep', 'dp'), split_axis=0, concat_axis=0, tile...]
    unnamed x15 -> x16, local copies, waits for them, and re-layouts: 3.75 us -> 22 us
    scatter x2 -> x0, local copies, waits for them, and re-layouts: 12.5 us -> none  [the longest x1 8.78 us: on_device(): jnp.zeros((experts * capacity, width), jnp.bfloat16).at[place].set(repeated)]
  transfers between devices with their start and end apart: 4 -> 0, of which waited for: 2 -> 0; matrix products, arithmetic and copies ran while one was open for 9% -> 0% of each run, Pallas kernels for 0% -> 0%
where the time goes in v1:
time: 175 us
  Pallas kernels  150 us (86%)
  local copies, waits for them, and re-layouts  23.5 us (13%)
    pallas_call x1, Pallas kernels, on_device(): pl.pallas_call(functools.partial(kernel, n_ep, n_dp, cap), out_shape=(jax...  150 us
    unnamed x16, local copies, waits for them, and re-layouts  22 us

profile of v1, /device:TPU:0, one launch (start us, length us, event | category | flops | bytes accessed | tf_op | source)
XLA Modules:
  0.0 174.6 jit_solution(3592102915896586603)
XLA Ops:
  0.6 0.0 copy-start
  0.6 1.5 broadcast_in_dim.9.gain_ref
  2.1 1.4 copy.15.ids_ref
  3.5 2.3 %copy.13.res_ref = bf16[128,2880]{1,0:T(8,128)(2,1)} copy(bf16[128,2880]{0,1:T(8,128)(2,1)} %param.7) | data formatting | bytes 1474560 | tf_op args[0]
  5.8 2.3 %copy.14.og_ref = bf16[128,2880]{1,0:T(8,128)(2,1)} copy(bf16[128,2880]{0,1:T(8,128)(2,1)} %param.10) | data formatting | bytes 1474560 | tf_op args[3]
  8.1 0.0 copy-done
  8.1 2.4 %copy.12 = bf16[1,768,1440]{2,1,0:T(8,128)(2,1)} copy(bf16[1,768,1440]{1,2,0:T(8,128)(2,1)S(1)} %copy-done) | data formatting | bytes 4423680 | tf_op args[5]
  10.5 149.8 %expert_backward.1 = (bf16[768,1440]{1,0:T(8,128)(2,1)}, bf16[1440,2880]{1,0:T(8,128)(2,1)}, bf16[128,2880]{1,0:T(8,128)(2,1)}, f32[32,2880]{1,0:T(8,128)}, f32[1,2880]{1,0:T(1,128)}) custom-call(bf16[128,2880]{1,0:T(8,128)(2,1)} %copy.13.res_ref, f32[1,2880]{1,0:T(1,128)} %broadcast_in_dim.9.gain_ref, bf16[32,2880]{1,0:T(8,128)(2,1)} %bitcast.11, ...), custom_call_target="tpu_custom_call" | custom-call | tf_op jit(solution)/shard_map/expert_backward/pallas_call | solution.py:275
  160.3 0.0 copy-start.3
  160.3 0.0 copy-start.1
  160.3 4.3 %copy.16 = bf16[1,768,1440]{1,2,0:T(8,128)(2,1)} copy(bf16[1,768,1440]{2,1,0:T(8,128)(2,1)} %bitcast.9) | data formatting | bytes 4423680
  164.6 0.0 copy-done.3
  164.6 0.6 reduce
  165.2 0.0 copy-done.1
  165.2 1.1 copy.17
  166.4 0.0 copy-start.2
  166.4 7.5 %copy.20 = bf16[1,1440,2880]{2,1,0:T(8,128)(2,1)} copy(bf16[1,1440,2880]{2,1,0:T(8,128)(2,1)} %bitcast.8) | data formatting | bytes 16588800
  173.8 0.0 copy-done.2
  173.9 0.7 copy.21
Async XLA Ops:
  0.6 7.4 %copy-start = (bf16[1,768,1440]{1,2,0:T(8,128)(2,1)S(1)}, bf16[1,768,1440]{1,2,0:T(8,128)(2,1)}, u32[]{:S(2)}) copy-start(bf16[1,768,1440]{1,2,0:T(8,128)(2,1)} %param.12) | copy-start | bytes 6635524
  160.3 4.3 %copy-start.3 = (f32[1,2880]{1,0:T(1,128)S(1)}, f32[1,2880]{1,0:T(1,128)}, u32[]{:S(2)}) copy-start(f32[1,2880]{1,0:T(1,128)} %get-tuple-element.14) | copy-start | bytes 34564
  160.3 4.9 %copy-start.1 = (bf16[128,2880]{1,0:T(8,128)(2,1)S(1)}, bf16[128,2880]{1,0:T(8,128)(2,1)}, u32[]{:S(2)}) copy-start(bf16[128,2880]{1,0:T(8,128)(2,1)} %get-tuple-element.17) | copy-start | bytes 2211844
  166.4 7.5 %copy-start.2 = (f32[32,2880]{1,0:T(8,128)S(1)}, f32[32,2880]{1,0:T(8,128)}, u32[]{:S(2)}) copy-start(f32[32,2880]{1,0:T(8,128)} %get-tuple-element.13) | copy-start | bytes 1105924

commit v2 on v1

--- a/solution.py
+++ b/solution.py
@@ -1,4 +1,5 @@
 import functools
+import math
 
 import jax
 import jax.numpy as jnp
@@ -9,25 +10,27 @@
 
 F32 = jnp.float32
 BF16 = jnp.bfloat16
+LINE = 4
 
 
 def kernel(
-    n_ep, n_dp, cap,
+    n_ep, n_dp, lines, cap,
     res_ref, gain_ref, rwt_ref, og_ref, ids_ref, hid_any, w_any,
     hg_any, wg_any, rg_ref, rgt_ref, gg_ref,
-    send, recv, w, hid, hidt, scaled, hg, wg, normed_s, unit_s, inv_s, prob_s, rank_s, rankt_s, probt_s,
+    tok, meta, metat, send, recv, w, hid, hidt, scaled, hg, wg, normed_s, unit_s, inv_s, prob_s, rank_s,
     ssend, srecv, part, rsbuf, agbuf,
-    in_sem, row_send, row_recv, sc_send, sc_recv, rs_send, rs_recv, ag_send, ag_recv, hg_sem, wg_sem,
+    in_sem, tok_send, tok_recv, meta_send, meta_recv, row_send, row_recv, sc_send, sc_recv, rs_send, rs_recv, ag_send, ag_recv, hg_sem, wg_sem,
 ):
     n = n_ep * n_dp
     tokens, width = res_ref.shape
     experts = rwt_ref.shape[0]
     ff = w.shape[0]
     pad_width = send.shape[2]
-    group = n_dp * cap
-    ep = lax.axis_index("ep")
-    dp = lax.axis_index("dp")
-    me = ep * n_dp + dp
+    plane = n // lines
+    group = plane * cap
+    me = lax.axis_index("ep") * n_dp + lax.axis_index("dp")
+    z = me // plane
+    p = me % plane
 
     def remote(src, dst, s_sem, r_sem, dev_ep, dev_dp):
         return pltpu.make_async_remote_copy(
@@ -75,101 +78,146 @@
     rank = jnp.where(match > 0, rank, F32(-1.0))
     prob_s[...] = prob
     rank_s[...] = rank
-    rankt_s[...] = rank.T.reshape(experts, 1, tokens)
-    probt_s[...] = prob.T.reshape(experts, 1, tokens)
+    tok[z] = og_ref[...]
+    meta[z] = jnp.concatenate([rank.T, prob.T], 0).astype(BF16)
 
     pl.semaphore_wait(barrier, n - 1)
 
-    def pack(g, _):
-        to = lax.rem(ep + n_ep - 1 - g, n_ep)
-        first = to * n_dp
-        rt = rankt_s[pl.ds(first, n_dp)]
-        pt = probt_s[pl.ds(first, n_dp)]
-        slot = lax.broadcasted_iota(jnp.int32, (n_dp, cap, tokens), 1).astype(F32)
+    def along(src, source, side):
+        to = (z + 2 * side - 1) * plane + p
+        return (
+            remote(src, tok.at[source], tok_send.at[source, side], tok_recv.at[source], to // n_dp, to % n_dp),
+            remote(
+                meta.at[source], meta.at[source], meta_send.at[source, side], meta_recv.at[source],
+                to // n_dp, to % n_dp,
+            ),
+        )
+
+    def start_along(src, source, side):
+        nxt = z + 2 * side - 1
+
+        @pl.when((nxt >= 0) & (nxt < lines))
+        def _():
+            for c in along(src, source, side):
+                c.start()
+
+    start_along(og_ref, z, 0)
+    start_along(og_ref, z, 1)
+
+    def sides(k, fn):
+        def step(i, _):
+            source = z + k * (2 * i - 1)
+
+            @pl.when((source >= 0) & (source < lines) & (k + 1 - i > 0) & (k >= 0))
+            def _():
+                fn(source, i)
+            return 0
+        lax.fori_loop(0, 2, step, 0)
+
+    def forward(source, i):
+        for c in along(tok.at[source], source, i):
+            c.wait_recv()
+        start_along(tok.at[source], source, 1 - i)
+
+    def pack(source, _):
+        metat[...] = meta[source].astype(F32).reshape(2 * experts, 1, tokens)
+        rt = metat[pl.ds(z * plane, plane)]
+        pt = metat[pl.ds(experts + z * plane, plane)]
+        slot = lax.broadcasted_iota(jnp.int32, (plane, cap, tokens), 1).astype(F32)
         hit = slot == rt
         hot = jnp.where(hit, F32(1.0), F32(0.0)).reshape(group, tokens).astype(BF16)
         weight = jnp.sum(jnp.where(hit, pt, F32(0.0)), -1, keepdims=True)
-        rows = jnp.dot(hot, og_ref[...], preferred_element_type=F32)
-        send[pl.ds(first, n_dp), :, pl.ds(0, width)] = rows.reshape(n_dp, cap, width).astype(BF16)
-        send[pl.ds(first, n_dp), :, pl.ds(width, pad_width - width)] = jnp.broadcast_to(
-            weight, (n_dp, cap, pad_width - width)
+        rows = jnp.dot(hot, tok[source], preferred_element_type=F32)
+        first = source * plane
+        send[pl.ds(first, plane), :, pl.ds(0, width)] = rows.reshape(plane, cap, width).astype(BF16)
+        send[pl.ds(first, plane), :, pl.ds(width, pad_width - width)] = jnp.broadcast_to(
+            weight, (plane, cap, pad_width - width)
         ).astype(BF16)
-        for k in range(n_dp):
-            j = lax.rem(dp + k, n_dp)
-            e = first + j
-
-            @pl.when(e != me)
-            def _():
-                remote(
-                    send.at[e], recv.at[me], row_send.at[e], row_recv.at[me], to, j
-                ).start()
-
-            @pl.when(e == me)
-            def _():
-                recv[me] = send[me]
-        return 0
-
-    lax.fori_loop(0, n_ep, pack, 0)
-
-    load_h.wait()
-    hidt[...] = hid[...].T
-    load_w.wait()
-
-    def wait_rows(src_ep):
-        for k in range(n_dp):
-            s = src_ep * n_dp + k
-
-            @pl.when(s != me)
-            def _():
-                remote(send.at[s], recv.at[s], row_send.at[s], row_recv.at[s], src_ep, k).wait_recv()
-
-    def take(src_ep):
-        got = recv[pl.ds(src_ep * n_dp, n_dp)].astype(F32)
-        return got.reshape(group, pad_width)
-
-    def chunk(c, _):
-        sources = (
-            lax.rem(ep + 1 + 2 * c, n_ep),
-            lax.rem(ep + 2 + 2 * c, n_ep),
-        )
-        for s in sources:
-            wait_rows(s)
-        rows = jnp.concatenate([take(s) for s in sources], 0)
-        starts = [pl.multiple_of(s * group, group) for s in sources]
-        h = jnp.concatenate([hid[pl.ds(b, group)] for b in starts], 0).astype(F32)
+        own = first + p
+        recv[own] = send[own]
+
+        def push(k, _):
+            q = (p + k) % plane
+            row_copy(first, z * plane + q, q).start()
+            return 0
+
+        lax.fori_loop(1, plane, push, 0)
+
+    def row_copy(first, to, q):
+        return remote(
+            send.at[first + q], recv.at[first + p], row_send.at[first + q], row_recv.at[first + p],
+            to // n_dp, to % n_dp,
+        )
+
+    def wait_row(first, q):
+        to = z * plane + q
+        return remote(
+            send.at[first + q], recv.at[first + q], row_send.at[first + q], row_recv.at[first + q],
+            to // n_dp, to % n_dp,
+        )
+
+    def chunk(source, _):
+        first = source * plane
+
+        def arrive(k, _):
+            wait_row(first, (p + k) % plane).wait_recv()
+            return 0
+
+        lax.fori_loop(1, plane, arrive, 0)
+        rows = recv[pl.ds(first, plane)].astype(F32).reshape(group, pad_width)
+        at = pl.ds(pl.multiple_of(first * cap, group), group)
+        h = hid[at].astype(F32)
         grad = rows[:, :width]
         weight = rows[:, width : width + 1]
         inner = lax.dot_general(
             grad.astype(BF16), w[...], (((1,), (1,)), ((), ())), preferred_element_type=F32
         )
-        score = jnp.sum(inner * h, -1, keepdims=True).reshape(2 * n_dp, cap, 1)
-        at_row = lax.broadcasted_iota(jnp.int32, (2 * n_dp, cap, 128), 1)
-        at_lane = lax.broadcasted_iota(jnp.int32, (2 * n_dp, cap, 128), 2)
-        score = jnp.sum(jnp.where(at_row == at_lane, score, F32(0.0)), 1, keepdims=True)
-        for i, s in enumerate(sources):
-            ssend[pl.ds(s * n_dp, n_dp)] = score[i * n_dp : (i + 1) * n_dp]
-            for k in range(n_dp):
-                d = s * n_dp + k
-
-                @pl.when(d != me)
-                def _():
-                    remote(ssend.at[d], srecv.at[me], sc_send.at[d], sc_recv.at[me], s, k).start()
-
-                @pl.when(d == me)
-                def _():
-                    srecv[me] = ssend[me]
-
-        hgrad = (weight * inner).astype(BF16)
-        scale = (weight * grad).astype(BF16)
-        for i, s in enumerate(sources):
-            hg[pl.ds(starts[i], group)] = hgrad[i * group : (i + 1) * group]
-            scaled[pl.ds(starts[i], group)] = scale[i * group : (i + 1) * group]
-            pltpu.make_async_copy(
-                hg.at[pl.ds(starts[i], group)], hg_any.at[pl.ds(starts[i], group)], hg_sem.at[s]
-            ).start()
-        return 0
-
-    lax.fori_loop(0, n_ep // 2, chunk, 0)
+        score = jnp.sum(inner * h, -1, keepdims=True).reshape(plane, cap, 1)
+        at_row = lax.broadcasted_iota(jnp.int32, (plane, cap, 128), 1)
+        at_lane = lax.broadcasted_iota(jnp.int32, (plane, cap, 128), 2)
+        ssend[pl.ds(first, plane)] = jnp.sum(
+            jnp.where(at_row == at_lane, score, F32(0.0)), 1, keepdims=True
+        )
+
+        def push(k, _):
+            d = first + k
+
+            @pl.when(d != me)
+            def _():
+                remote(
+                    ssend.at[d], srecv.at[me], sc_send.at[d], sc_recv.at[me], d // n_dp, d % n_dp
+                ).start()
+            return 0
+
+        lax.fori_loop(0, plane, push, 0)
+
+        @pl.when(source == z)
+        def _():
+            srecv[me] = ssend[me]
+
+        hg[at] = (weight * inner).astype(BF16)
+        scaled[at] = (weight * grad).astype(BF16)
+        pltpu.make_async_copy(hg.at[at], hg_any.at[at], hg_sem.at[source]).start()
+
+    def stage(k, _):
+        @pl.when((k > 0) & (k < lines))
+        def _():
+            sides(k, forward)
+
+        @pl.when(k < lines)
+        def _():
+            sides(k, pack)
+
+        @pl.when(k == 0)
+        def _():
+            load_h.wait()
+            hidt[...] = hid[...].T
+            load_w.wait()
+
+        sides(k - 1, chunk)
+        return 0
+
+    lax.fori_loop(0, lines + 1, stage, 0)
 
     blocks = wg_sem.shape[0]
     rows_of = ff // blocks
@@ -232,19 +280,44 @@
     gg_ref[...] = jnp.sum(total * rwt.astype(F32), 0, keepdims=True) / gain_ref[...]
 
     def finish(i):
-        remote(send.at[i], recv.at[me], row_send.at[i], row_recv.at[me], i // n_dp, i % n_dp).wait_send()
         remote(ssend.at[i], srecv.at[me], sc_send.at[i], sc_recv.at[me], i // n_dp, i % n_dp).wait_send()
         remote(part.at[i], rsbuf.at[me], rs_send.at[i], rs_recv.at[me], i // n_dp, i % n_dp).wait_send()
         remote(agbuf.at[me], agbuf.at[me], ag_send.at[i], ag_recv.at[me], i // n_dp, i % n_dp).wait_send()
 
     others(finish)
 
+    def finish_rows(source, _):
+        def step(k, _):
+            q = (p + k) % plane
+            row_copy(source * plane, z * plane + q, q).wait_send()
+            return 0
+        lax.fori_loop(1, plane, step, 0)
+
+        def sent(side):
+            nxt = z + 2 * side - 1
+
+            @pl.when((nxt >= 0) & (nxt < lines))
+            def _():
+                for c in along(tok.at[source], source, side):
+                    c.wait_send()
+
+        @pl.when(source <= z)
+        def _():
+            sent(1)
+
+        @pl.when(source >= z)
+        def _():
+            sent(0)
+        return 0
+
+    lax.fori_loop(0, lines, finish_rows, 0)
+
     def drain_h(g, _):
         at = pl.ds(pl.multiple_of(g * group, group), group)
         pltpu.make_async_copy(hg.at[at], hg_any.at[at], hg_sem.at[g]).wait()
         return 0
 
-    lax.fori_loop(0, n_ep, drain_h, 0)
+    lax.fori_loop(0, lines, drain_h, 0)
 
     def drain_w(b, _):
         at = pl.ds(pl.multiple_of(b * rows_of, rows_of), rows_of)
@@ -256,6 +329,7 @@
 
 def on_device(n_ep, n_dp, residual, norm_gain, router_weight, out_grad, expert_ids, hidden, down_weight):
     n = n_ep * n_dp
+    lines = math.gcd(n_ep, LINE)
     tokens, width = residual.shape
     experts = router_weight.shape[1]
     slots, ff = hidden.shape[1:]
@@ -273,7 +347,7 @@
     anyspace = pl.BlockSpec(memory_space=pl.ANY)
     dma = pltpu.SemaphoreType.DMA
     hg, wg, rg, rgt, gg = pl.pallas_call(
-        functools.partial(kernel, n_ep, n_dp, cap),
+        functools.partial(kernel, n_ep, n_dp, lines, cap),
         out_shape=(
             jax.ShapeDtypeStruct((rows, ff), BF16),
             jax.ShapeDtypeStruct((ff, width), BF16),
@@ -284,6 +358,9 @@
         in_specs=[vmem] * 5 + [anyspace] * 2,
         out_specs=(anyspace, anyspace, vmem, vmem, vmem),
         scratch_shapes=[
+            pltpu.VMEM((lines, tokens, width), BF16),
+            pltpu.VMEM((lines, 2 * experts, tokens), BF16),
+            pltpu.VMEM((2 * experts, 1, tokens), F32),
             pltpu.VMEM((n, cap, pad_width), BF16),
             pltpu.VMEM((n, cap, pad_width), BF16),
             pltpu.VMEM((ff, width), BF16),
@@ -297,21 +374,20 @@
             pltpu.VMEM((tokens, 1), F32),
             pltpu.VMEM((tokens, experts), F32),
             pltpu.VMEM((tokens, experts), F32),
-            pltpu.VMEM((experts, 1, tokens), F32),
-            pltpu.VMEM((experts, 1, tokens), F32),
             pltpu.VMEM((n, 1, 128), F32),
             pltpu.VMEM((n, 1, 128), F32),
             pltpu.VMEM((n, 1, width), F32),
             pltpu.VMEM((n, 1, width), F32),
             pltpu.VMEM((n, 1, width), F32),
             dma((2,)),
+            dma((lines, 2)), dma((lines,)), dma((lines, 2)), dma((lines,)),
             dma((n,)), dma((n,)), dma((n,)), dma((n,)),
             dma((n,)), dma((n,)), dma((n,)), dma((n,)),
-            dma((n_ep,)),
+            dma((lines,)),
             dma((blocks,)),
         ],
         compiler_params=pltpu.CompilerParams(
-            collective_id=0, has_side_effects=True, vmem_limit_bytes=60 * 1024 * 1024
+            collective_id=0, has_side_effects=True, vmem_limit_bytes=67_000_000
         ),
         name="expert_backward",
     )(residual, norm_gain[None], router_weight.T, out_grad, expert_ids, hid, down_weight[0])

time: 175 us -> 131 us (0.75); the launches traced: 175 us -> 129 us
  Pallas kernels: 150 us -> 104 us
    pallas_call x1, Pallas kernels: 150 us -> 104 us  [on_device(): pl.pallas_call(functools.partial(kernel, n_ep, n_dp, lines, cap), out_sha...]
where the time goes in v2:
time: 131 us; the launch traced here: 129 us
  Pallas kernels  104 us (79%)
  local copies, waits for them, and re-layouts  23.5 us (18%)
    pallas_call x1, Pallas kernels, on_device(): pl.pallas_call(functools.partial(kernel, n_ep, n_dp, lines, cap), out_sha...  104 us
    unnamed x16, local copies, waits for them, and re-layouts  22 us

profile of v2, /device:TPU:0, one launch (start us, length us, event | category | flops | bytes accessed | tf_op | source)
XLA Modules:
  0.0 128.8 jit_solution(16711710579781621034)
XLA Ops:
  0.6 0.0 copy-start
  0.6 1.5 %broadcast_in_dim.9.gain_ref = f32[1,2880]{1,0:T(1,128)} reshape(f32[2880]{0:T(1024)} %param.8) | data formatting | bytes 23040 | tf_op jit(solution)/shard_map/broadcast_in_dim | solution.py:393
  2.1 1.4 %copy.15.ids_ref = s32[128,4]{1,0:T(8,128)} copy(s32[128,4]{0,1:T(4,128)} %param.11) | data formatting | bytes 4096 | tf_op args[4]
  3.5 2.3 %copy.13.res_ref = bf16[128,2880]{1,0:T(8,128)(2,1)} copy(bf16[128,2880]{0,1:T(8,128)(2,1)} %param.7) | data formatting | bytes 1474560 | tf_op args[0]
  5.8 2.3 %copy.14.og_ref = bf16[128,2880]{1,0:T(8,128)(2,1)} copy(bf16[128,2880]{0,1:T(8,128)(2,1)} %param.10) | data formatting | bytes 1474560 | tf_op args[3]
  8.1 0.0 copy-done
  8.1 2.4 %copy.12 = bf16[1,768,1440]{2,1,0:T(8,128)(2,1)} copy(bf16[1,768,1440]{1,2,0:T(8,128)(2,1)S(1)} %copy-done) | data formatting | bytes 4423680 | tf_op args[5]
  10.5 104.0 %expert_backward.1 = (bf16[768,1440]{1,0:T(8,128)(2,1)}, bf16[1440,2880]{1,0:T(8,128)(2,1)}, bf16[128,2880]{1,0:T(8,128)(2,1)}, f32[32,2880]{1,0:T(8,128)}, f32[1,2880]{1,0:T(1,128)}) custom-call(bf16[128,2880]{1,0:T(8,128)(2,1)} %copy.13.res_ref, f32[1,2880]{1,0:T(1,128)} %broadcast_in_dim.9.gain_ref, bf16[32,2880]{1,0:T(8,128)(2,1)} %bitcast.11, ...), custom_call_target="tpu_custom_call" | custom-call | tf_op jit(solution)/shard_map/expert_backward/pallas_call | solution.py:349
  114.5 0.0 copy-start.3
  114.5 0.0 copy-start.1
  114.5 4.3 %copy.16 = bf16[1,768,1440]{1,2,0:T(8,128)(2,1)} copy(bf16[1,768,1440]{2,1,0:T(8,128)(2,1)} %bitcast.9) | data formatting | bytes 4423680
  118.8 0.0 copy-done.3
  118.8 0.6 reduce
  119.4 0.0 copy-done.1
  119.4 1.1 copy.17
  120.6 0.0 copy-start.2
  120.6 7.5 %copy.20 = bf16[1,1440,2880]{2,1,0:T(8,128)(2,1)} copy(bf16[1,1440,2880]{2,1,0:T(8,128)(2,1)} %bitcast.8) | data formatting | bytes 16588800
  128.0 0.0 copy-done.2
  128.0 0.7 copy.21
Async XLA Ops:
  0.6 7.4 %copy-start = (bf16[1,768,1440]{1,2,0:T(8,128)(2,1)S(1)}, bf16[1,768,1440]{1,2,0:T(8,128)(2,1)}, u32[]{:S(2)}) copy-start(bf16[1,768,1440]{1,2,0:T(8,128)(2,1)} %param.12) | copy-start | bytes 6635524
  114.5 4.3 %copy-start.3 = (f32[1,2880]{1,0:T(1,128)S(1)}, f32[1,2880]{1,0:T(1,128)}, u32[]{:S(2)}) copy-start(f32[1,2880]{1,0:T(1,128)} %get-tuple-element.14) | copy-start | bytes 34564
  114.5 4.9 %copy-start.1 = (bf16[128,2880]{1,0:T(8,128)(2,1)S(1)}, bf16[128,2880]{1,0:T(8,128)(2,1)}, u32[]{:S(2)}) copy-start(bf16[128,2880]{1,0:T(8,128)(2,1)} %get-tuple-element.17) | copy-start | bytes 2211844
  120.6 7.5 %copy-start.2 = (f32[32,2880]{1,0:T(8,128)S(1)}, f32[32,2880]{1,0:T(8,128)}, u32[]{:S(2)}) copy-start(f32[32,2880]{1,0:T(8,128)} %get-tuple-element.13) | copy-start | bytes 1105924

commit v3 on v2

--- a/solution.py
+++ b/solution.py
@@ -15,14 +15,14 @@
 
 def kernel(
     n_ep, n_dp, lines, cap,
-    res_ref, gain_ref, rwt_ref, og_ref, ids_ref, hid_any, w_any,
-    hg_any, wg_any, rg_ref, rgt_ref, gg_ref,
-    tok, meta, metat, send, recv, w, hid, hidt, scaled, hg, wg, normed_s, unit_s, inv_s, prob_s, rank_s,
+    res_ref, gain_ref, rwt_ref, og_ref, ids_ref, hidt_any, w_any,
+    hgt_any, wg_any, rg_ref, rgt_ref, gg_ref,
+    tok, meta, metat, send, recv, w, hid3, hidt, scaled, hg3, hgt, wg, normed_s, unit_s, inv_s, prob_s, rank_s,
     ssend, srecv, part, rsbuf, agbuf,
     in_sem, tok_send, tok_recv, meta_send, meta_recv, row_send, row_recv, sc_send, sc_recv, rs_send, rs_recv, ag_send, ag_recv, hg_sem, wg_sem,
 ):
     n = n_ep * n_dp
-    tokens, width = res_ref.shape
+    width, tokens = res_ref.shape
     experts = rwt_ref.shape[0]
     ff = w.shape[0]
     pad_width = send.shape[2]
@@ -49,37 +49,37 @@
         return 0
 
     lax.fori_loop(0, n, greet, 0)
-    load_h = pltpu.make_async_copy(hid_any, hid, in_sem.at[0])
+    load_h = pltpu.make_async_copy(hidt_any, hidt, in_sem.at[0])
     load_w = pltpu.make_async_copy(w_any, w, in_sem.at[1])
     load_h.start()
     load_w.start()
 
+    gain = jnp.broadcast_to(gain_ref[...], (tokens, width)).T
+    ssend[...] = jnp.zeros_like(ssend)
     floated = res_ref[...].astype(F32)
-    inverse = lax.rsqrt(jnp.mean(floated * floated, -1, keepdims=True) + 1e-05)
+    inverse = lax.rsqrt(jnp.mean(floated * floated, 0, keepdims=True) + 1e-05)
     unit = floated * inverse
-    normed = (unit * gain_ref[...]).astype(BF16)
+    normed = (unit * gain).astype(BF16)
     unit_s[...] = unit
     inv_s[...] = inverse
     normed_s[...] = normed
-    logits = lax.dot_general(
-        normed, rwt_ref[...], (((1,), (1,)), ((), ())), preferred_element_type=F32
-    )
-    lane_e = lax.broadcasted_iota(jnp.int32, (tokens, experts), 1)
-    match = jnp.zeros((tokens, experts), F32)
+    logits = jnp.dot(rwt_ref[...], normed, preferred_element_type=F32)
+    row_e = lax.broadcasted_iota(jnp.int32, (experts, tokens), 0)
+    match = jnp.zeros((experts, tokens), F32)
     ids = ids_ref[...]
-    for k in range(ids.shape[1]):
-        match = match + jnp.where(ids[:, k : k + 1] == lane_e, F32(1.0), F32(0.0))
+    for k in range(ids.shape[0]):
+        match = match + jnp.where(ids[k : k + 1, :] == row_e, F32(1.0), F32(0.0))
     expo = jnp.where(match > 0, jnp.exp(logits), F32(0.0))
-    prob = expo / jnp.sum(expo, -1, keepdims=True)
+    prob = expo / jnp.sum(expo, 0, keepdims=True)
     row_t = lax.broadcasted_iota(jnp.int32, (tokens, tokens), 0)
     col_t = lax.broadcasted_iota(jnp.int32, (tokens, tokens), 1)
-    lower = jnp.where(col_t < row_t, F32(1.0), F32(0.0)).astype(BF16)
-    rank = jnp.dot(lower, match.astype(BF16), preferred_element_type=F32)
+    before = jnp.where(row_t < col_t, F32(1.0), F32(0.0)).astype(BF16)
+    rank = jnp.dot(match.astype(BF16), before, preferred_element_type=F32)
     rank = jnp.where(match > 0, rank, F32(-1.0))
     prob_s[...] = prob
     rank_s[...] = rank
     tok[z] = og_ref[...]
-    meta[z] = jnp.concatenate([rank.T, prob.T], 0).astype(BF16)
+    meta[z] = jnp.concatenate([rank, prob], 0).astype(BF16)
 
     pl.semaphore_wait(barrier, n - 1)
 
@@ -127,7 +127,9 @@
         hit = slot == rt
         hot = jnp.where(hit, F32(1.0), F32(0.0)).reshape(group, tokens).astype(BF16)
         weight = jnp.sum(jnp.where(hit, pt, F32(0.0)), -1, keepdims=True)
-        rows = jnp.dot(hot, tok[source], preferred_element_type=F32)
+        rows = lax.dot_general(
+            hot, tok[source], (((1,), (1,)), ((), ())), preferred_element_type=F32
+        )
         first = source * plane
         send[pl.ds(first, plane), :, pl.ds(0, width)] = rows.reshape(plane, cap, width).astype(BF16)
         send[pl.ds(first, plane), :, pl.ds(width, pad_width - width)] = jnp.broadcast_to(
@@ -166,18 +168,15 @@
         lax.fori_loop(1, plane, arrive, 0)
         rows = recv[pl.ds(first, plane)].astype(F32).reshape(group, pad_width)
         at = pl.ds(pl.multiple_of(first * cap, group), group)
-        h = hid[at].astype(F32)
+        h = hid3[source].astype(F32)
         grad = rows[:, :width]
         weight = rows[:, width : width + 1]
         inner = lax.dot_general(
-            grad.astype(BF16), w[...], (((1,), (1,)), ((), ())), preferred_element_type=F32
-        )
-        score = jnp.sum(inner * h, -1, keepdims=True).reshape(plane, cap, 1)
-        at_row = lax.broadcasted_iota(jnp.int32, (plane, cap, 128), 1)
-        at_lane = lax.broadcasted_iota(jnp.int32, (plane, cap, 128), 2)
-        ssend[pl.ds(first, plane)] = jnp.sum(
-            jnp.where(at_row == at_lane, score, F32(0.0)), 1, keepdims=True
-        )
+            w[...], grad.astype(BF16), (((1,), (1,)), ((), ())), preferred_element_type=F32
+        )
+        score = jnp.sum(inner * h, 0, keepdims=True)
+        for k in range(plane):
+            ssend[first + k, :, pl.ds(0, cap)] = score[:, k * cap : (k + 1) * cap]
 
         def push(k, _):
             d = first + k
@@ -195,9 +194,9 @@
         def _():
             srecv[me] = ssend[me]
 
-        hg[at] = (weight * inner).astype(BF16)
+        across = jnp.broadcast_to(weight, (group, 128)).T[0:1, :]
+        hg3[source] = (across * inner).astype(BF16)
         scaled[at] = (weight * grad).astype(BF16)
-        pltpu.make_async_copy(hg.at[at], hg_any.at[at], hg_sem.at[source]).start()
 
     def stage(k, _):
         @pl.when((k > 0) & (k < lines))
@@ -211,7 +210,8 @@
         @pl.when(k == 0)
         def _():
             load_h.wait()
-            hidt[...] = hid[...].T
+            for i in range(lines):
+                hid3[i] = hidt[:, i * group : (i + 1) * group]
             load_w.wait()
 
         sides(k - 1, chunk)
@@ -219,13 +219,26 @@
 
     lax.fori_loop(0, lines + 1, stage, 0)
 
+    for i in range(lines):
+        hgt[:, i * group : (i + 1) * group] = hg3[i]
+    store_h = pltpu.make_async_copy(hgt, hgt_any, hg_sem)
+    store_h.start()
+
     blocks = wg_sem.shape[0]
     rows_of = ff // blocks
 
+    def wg_copy(b):
+        at = pl.ds(pl.multiple_of(b * rows_of, rows_of), rows_of)
+        return pltpu.make_async_copy(wg.at[b % 2], wg_any.at[at], wg_sem.at[b])
+
     def wg_block(b, _):
+        @pl.when(b >= 2)
+        def _():
+            wg_copy(b - 2).wait()
+
         at = pl.ds(pl.multiple_of(b * rows_of, rows_of), rows_of)
-        wg[at] = jnp.dot(hidt[at], scaled[...], preferred_element_type=F32).astype(BF16)
-        pltpu.make_async_copy(wg.at[at], wg_any.at[at], wg_sem.at[b]).start()
+        wg[b % 2] = jnp.dot(hidt[at], scaled[...], preferred_element_type=F32).astype(BF16)
+        wg_copy(b).start()
         return 0
 
     def others(fn):
@@ -240,17 +253,19 @@
     lax.fori_loop(0, cut1, wg_block, 0)
 
     others(lambda i: remote(ssend.at[i], srecv.at[i], sc_send.at[i], sc_recv.at[i], i // n_dp, i % n_dp).wait_recv())
-    back = srecv[...].reshape(n, 128).T
+    back = srecv[...].reshape(n, 128)
     rank = rank_s[...]
     prob = prob_s[...]
-    score = jnp.zeros((tokens, experts), F32)
+    score = jnp.zeros((experts, tokens), F32)
     for r in range(cap):
-        score = score + jnp.where(rank == F32(r), back[r : r + 1, :], F32(0.0))
-    lg = prob * (score - jnp.sum(prob * score, -1, keepdims=True))
-    lgt = lg.T
-    hit = lgt.astype(BF16)
-    lot = (lgt - hit.astype(F32)).astype(BF16)
-    both = jnp.dot(jnp.concatenate([hit, lot], 0), normed_s[...], preferred_element_type=F32)
+        score = score + jnp.where(rank == F32(r), back[:, r : r + 1], F32(0.0))
+    lg = prob * (score - jnp.sum(prob * score, 0, keepdims=True))
+    hi = lg.astype(BF16)
+    lo = (lg - hi.astype(F32)).astype(BF16)
+    both = lax.dot_general(
+        jnp.concatenate([hi, lo], 0), normed_s[...], (((1,), (1,)), ((), ())),
+        preferred_element_type=F32,
+    )
     router = both[:experts] + both[experts:]
     for e in range(experts):
         part[e] = router[e : e + 1, :]
@@ -263,13 +278,14 @@
     agbuf[me] = jnp.sum(rsbuf[...], 0)
     others(lambda i: remote(agbuf.at[me], agbuf.at[me], ag_send.at[i], ag_recv.at[me], i // n_dp, i % n_dp).start())
 
-    hi = lg.astype(BF16)
-    lo = (lg - hi.astype(F32)).astype(BF16)
     rwt = rwt_ref[...]
-    ngrad = jnp.dot(hi, rwt, preferred_element_type=F32) + jnp.dot(lo, rwt, preferred_element_type=F32)
-    upper = ngrad * gain_ref[...]
+    ngrad = lax.dot_general(
+        jnp.concatenate([rwt, rwt], 0), jnp.concatenate([hi, lo], 0), (((0,), (0,)), ((), ())),
+        preferred_element_type=F32,
+    )
+    upper = ngrad * jnp.broadcast_to(gain_ref[...], (tokens, width)).T
     unit = unit_s[...]
-    mean = jnp.mean(upper * unit, -1, keepdims=True)
+    mean = jnp.mean(upper * unit, 0, keepdims=True)
     rg_ref[...] = (inv_s[...] * (upper - unit * mean)).astype(BF16)
 
     lax.fori_loop(cut2, blocks, wg_block, 0)
@@ -312,19 +328,9 @@
 
     lax.fori_loop(0, lines, finish_rows, 0)
 
-    def drain_h(g, _):
-        at = pl.ds(pl.multiple_of(g * group, group), group)
-        pltpu.make_async_copy(hg.at[at], hg_any.at[at], hg_sem.at[g]).wait()
-        return 0
-
-    lax.fori_loop(0, lines, drain_h, 0)
-
-    def drain_w(b, _):
-        at = pl.ds(pl.multiple_of(b * rows_of, rows_of), rows_of)
-        pltpu.make_async_copy(wg.at[at], wg_any.at[at], wg_sem.at[b]).wait()
-        return 0
-
-    lax.fori_loop(0, blocks, drain_w, 0)
+    store_h.wait()
+    for b in range(max(0, blocks - 2), blocks):
+        wg_copy(b).wait()
 
 
 def on_device(n_ep, n_dp, residual, norm_gain, router_weight, out_grad, expert_ids, hidden, down_weight):
@@ -336,44 +342,45 @@
     real_cap = slots // experts
     cap = -(-real_cap // 8) * 8
     pad_width = -(-(width + 1) // 128) * 128
-    hid = hidden[0]
+    hidt = hidden[0].T
     if cap != real_cap:
-        hid = jnp.pad(
-            hid.reshape(experts, real_cap, ff), ((0, 0), (0, cap - real_cap), (0, 0))
-        ).reshape(experts * cap, ff)
+        hidt = jnp.pad(
+            hidt.reshape(ff, experts, real_cap), ((0, 0), (0, 0), (0, cap - real_cap))
+        ).reshape(ff, experts * cap)
     rows = experts * cap
     blocks = max(b for b in range(1, 6) if ff % (b * 16) == 0)
     vmem = pl.BlockSpec(memory_space=pltpu.VMEM)
     anyspace = pl.BlockSpec(memory_space=pl.ANY)
     dma = pltpu.SemaphoreType.DMA
-    hg, wg, rg, rgt, gg = pl.pallas_call(
+    hgt, wg, rg, rgt, gg = pl.pallas_call(
         functools.partial(kernel, n_ep, n_dp, lines, cap),
         out_shape=(
-            jax.ShapeDtypeStruct((rows, ff), BF16),
+            jax.ShapeDtypeStruct((ff, rows), BF16),
             jax.ShapeDtypeStruct((ff, width), BF16),
-            jax.ShapeDtypeStruct((tokens, width), BF16),
+            jax.ShapeDtypeStruct((width, tokens), BF16),
             jax.ShapeDtypeStruct((experts, width), F32),
             jax.ShapeDtypeStruct((1, width), F32),
         ),
         in_specs=[vmem] * 5 + [anyspace] * 2,
         out_specs=(anyspace, anyspace, vmem, vmem, vmem),
         scratch_shapes=[
-            pltpu.VMEM((lines, tokens, width), BF16),
+            pltpu.VMEM((lines, width, tokens), BF16),
             pltpu.VMEM((lines, 2 * experts, tokens), BF16),
             pltpu.VMEM((2 * experts, 1, tokens), F32),
             pltpu.VMEM((n, cap, pad_width), BF16),
             pltpu.VMEM((n, cap, pad_width), BF16),
             pltpu.VMEM((ff, width), BF16),
-            pltpu.VMEM((rows, ff), BF16),
+            pltpu.VMEM((lines, ff, rows // lines), BF16),
             pltpu.VMEM((ff, rows), BF16),
             pltpu.VMEM((rows, width), BF16),
-            pltpu.VMEM((rows, ff), BF16),
-            pltpu.VMEM((ff, width), BF16),
-            pltpu.VMEM((tokens, width), BF16),
-            pltpu.VMEM((tokens, width), F32),
-            pltpu.VMEM((tokens, 1), F32),
-            pltpu.VMEM((tokens, experts), F32),
-            pltpu.VMEM((tokens, experts), F32),
+            pltpu.VMEM((lines, ff, rows // lines), BF16),
+            pltpu.VMEM((ff, rows), BF16),
+            pltpu.VMEM((2, ff // blocks, width), BF16),
+            pltpu.VMEM((width, tokens), BF16),
+            pltpu.VMEM((width, tokens), F32),
+            pltpu.VMEM((1, tokens), F32),
+            pltpu.VMEM((experts, tokens), F32),
+            pltpu.VMEM((experts, tokens), F32),
             pltpu.VMEM((n, 1, 128), F32),
             pltpu.VMEM((n, 1, 128), F32),
             pltpu.VMEM((n, 1, width), F32),
@@ -383,17 +390,17 @@
             dma((lines, 2)), dma((lines,)), dma((lines, 2)), dma((lines,)),
             dma((n,)), dma((n,)), dma((n,)), dma((n,)),
             dma((n,)), dma((n,)), dma((n,)), dma((n,)),
-            dma((lines,)),
+            dma,
             dma((blocks,)),
         ],
         compiler_params=pltpu.CompilerParams(
             collective_id=0, has_side_effects=True, vmem_limit_bytes=67_000_000
         ),
         name="expert_backward",
-    )(residual, norm_gain[None], router_weight.T, out_grad, expert_ids, hid, down_weight[0])
+    )(residual.T, norm_gain[None], router_weight.T, out_grad.T, expert_ids.T, hidt, down_weight[0])
     if cap != real_cap:
-        hg = hg.reshape(experts, cap, ff)[:, :real_cap].reshape(slots, ff)
-    return hg[None], wg[None], rg, rgt.T, gg[0]
+        hgt = hgt.reshape(ff, experts, cap)[:, :, :real_cap].reshape(ff, slots)
+    return hgt.T[None], wg[None], rg.T, rgt.T, gg[0]
 
 
 def solution(mesh):

time: 131 us -> 120 us (0.916); the launches traced: 129 us -> 119 us
  local copies, waits for them, and re-layouts: 23.5 us -> 13.6 us
    unnamed x16 -> x8, local copies, waits for them, and re-layouts: 22 us -> 12.2 us
where the time goes in v3:
time: 120 us; the launch traced here: 119 us
  Pallas kernels  104 us (87%)
  local copies, waits for them, and re-layouts  13.6 us (11%)
  other arithmetic  1.34 us (1%)
    pallas_call x1, Pallas kernels, on_device(): pl.pallas_call(functools.partial(kernel, n_ep, n_dp, lines, cap), out_sha...  104 us
    unnamed x8, local copies, waits for them, and re-layouts  12.2 us

profile of v3, /device:TPU:0, one launch (start us, length us, event | category | flops | bytes accessed | tf_op | source)
XLA Modules:
  0.0 119.1 jit_solution(13313513826478395642)
XLA Ops:
  0.6 1.3 %broadcast_in_dim.9.gain_ref = f32[1,2880]{1,0:T(1,128)} reshape(f32[2880]{0:T(1024)} %param.8) | data formatting | bytes 23040 | tf_op jit(solution)/shard_map/broadcast_in_dim | solution.py:400
  1.9 103.6 %expert_backward.1 = (bf16[1440,768]{1,0:T(8,128)(2,1)}, bf16[1440,2880]{1,0:T(8,128)(2,1)}, bf16[2880,128]{1,0:T(8,128)(2,1)}, f32[32,2880]{1,0:T(8,128)}, f32[1,2880]{1,0:T(1,128)}) custom-call(bf16[2880,128]{1,0:T(8,128)(2,1)} %bitcast.19, f32[1,2880]{1,0:T(1,128)} %broadcast_in_dim.9.gain_ref, bf16[32,2880]{1,0:T(8,128)(2,1)} %bitcast.22, ...), custom_call_target="tpu_custom_call" | custom-call | tf_op jit(solution)/shard_map/expert_backward/pallas_call | solution.py:355
  105.5 1.3 %reduce = f32[2880]{0:T(1024)} reduce(f32[1,2880]{1,0:T(1,128)} %get-tuple-element.14, f32[]{:T(128)} %constant.2), dimensions={0}, to_apply=%get-tuple-element.14.reduce_sub_computation | reduce | bytes 23044 | tf_op jit(solution)/shard_map/expert_backward/pallas_call | solution.py:355
  106.9 3.1 %copy.16 = bf16[1,768,1440]{1,2,0:T(8,128)(2,1)} copy(bf16[1,768,1440]{1,2,0:T(8,128)(2,1)} %bitcast.17) | data formatting | bytes 4423680
  110.0 0.0 copy-start
  110.0 0.0 copy-start.1
  110.0 7.5 %copy.17 = bf16[1,1440,2880]{2,1,0:T(8,128)(2,1)} copy(bf16[1,1440,2880]{2,1,0:T(8,128)(2,1)} %bitcast.15) | data formatting | bytes 16588800
  117.5 0.0 copy-done
  117.5 0.9 copy.18
  118.4 0.0 copy-done.1
  118.4 0.7 copy.19
Async XLA Ops:
  110.0 7.5 %copy-start = (bf16[2880,128]{1,0:T(8,128)(2,1)S(1)}, bf16[2880,128]{1,0:T(8,128)(2,1)}, u32[]{:S(2)}) copy-start(bf16[2880,128]{1,0:T(8,128)(2,1)} %get-tuple-element.12) | copy-start | bytes 2211844
  110.0 8.4 %copy-start.1 = (f32[32,2880]{1,0:T(8,128)S(1)}, f32[32,2880]{1,0:T(8,128)}, u32[]{:S(2)}) copy-start(f32[32,2880]{1,0:T(8,128)} %get-tuple-element.13) | copy-start | bytes 1105924
